TPU v7x, 16 devices: a whole 2x2x2 slice. The times are simulated.
16 devices in a mesh: stage: 2 (over z), data: 8 (over y, x, core).
Axes of the slice: x: 2, y: 2, z: 2, core: 2. Of those that a mesh axis runs over, the one named last changes fastest.
Arguments:
- tokens_in: bfloat16 [16, 512, 896], P('data')
- targets: bfloat16 [16, 512, 896], P('data')
- w_up: bfloat16 [2, 6, 896, 4864], P(None, 'stage')
- w_down: bfloat16 [2, 6, 4864, 896], P(None, 'stage')
Outputs:
- output 1: float32 [], replicated
- output 2: float32 [2, 6, 896, 4864], P(None, 'stage', 'data')
- output 3: float32 [2, 6, 4864, 896], P(None, 'stage', 'data')
All inputs are finite; a program needn't handle non-finite values.
Results may differ from a plain program's by a relative error of at most 0.00136694.
Values are sent between devices in bfloat16 or wider.
A program may use at most 1 GiB of HBM per device.

v0:
```python
import jax
import jax.numpy as jnp
from jax import lax
from jax.sharding import PartitionSpec as P


def gelu_fn(pre_act):
    return jax.nn.gelu(pre_act, approximate=True)


def layer_fwd(h_in, w_one, w_two):
    pre_act = jnp.dot(h_in, w_one, preferred_element_type=jnp.float32)
    act_bf = gelu_fn(pre_act).astype(jnp.bfloat16)
    out_val = h_in.astype(jnp.float32) + jnp.dot(act_bf, w_two, preferred_element_type=jnp.float32)
    return out_val.astype(jnp.bfloat16)


def layer_bwd(h_in, grad_out, w_one, w_two):
    pre_act = jnp.dot(h_in, w_one, preferred_element_type=jnp.float32)
    act_val, gelu_vjp = jax.vjp(gelu_fn, pre_act)
    act_bf = act_val.astype(jnp.bfloat16)
    g_down = jnp.einsum("tf,td->fd", act_bf, grad_out, preferred_element_type=jnp.float32)
    d_act = jnp.einsum("td,fd->tf", grad_out, w_two, preferred_element_type=jnp.float32).astype(jnp.bfloat16)
    d_pre = gelu_vjp(d_act.astype(jnp.float32))[0].astype(jnp.bfloat16)
    g_up = jnp.einsum("td,tf->df", h_in, d_pre, preferred_element_type=jnp.float32)
    back_val = jnp.einsum("tf,df->td", d_pre, w_one, preferred_element_type=jnp.float32)
    d_in = (grad_out.astype(jnp.float32) + back_val).astype(jnp.bfloat16)
    return d_in, g_up, g_down


def add_layer(acc_arr, new_part, layer_idx):
    start_idx = (layer_idx, 0, 0)
    old_val = lax.dynamic_slice(acc_arr, start_idx, (1,) + new_part.shape)
    return lax.dynamic_update_slice(acc_arr, old_val + new_part[None], start_idx)


def make_tick(n_stage, n_micro, n_tok, tokens_loc, targets_loc, up_loc, down_loc, with_top):
    block_len = up_loc.shape[1]
    n_slots = min(4 * n_stage, 2 * n_micro)
    cycle_len = 2 * n_stage
    stage_idx = lax.axis_index("stage")
    fwd_perm = [(src_dev, (src_dev + 1) % n_stage) for src_dev in range(n_stage)]
    bwd_perm = [(src_dev, (src_dev - 1) % n_stage) for src_dev in range(n_stage)]

    def tick(tick_idx, state):
        fwd_in, bwd_in, top_grad, act_stash, acc_list, loss_acc = state
        b_slot = tick_idx - 2 * n_stage - (n_stage - 1 - stage_idx)
        b_valid = (b_slot >= 0) & (b_slot < 2 * n_micro)
        b_slot = jnp.clip(b_slot, 0, 2 * n_micro - 1)
        b_rem = b_slot % cycle_len
        b_virt = 1 - b_rem // n_stage
        b_saved = (b_slot // cycle_len) * cycle_len + b_virt * n_stage + b_rem % n_stage
        saved_pos = b_saved % n_slots
        use_top = (stage_idx == n_stage - 1) & (b_virt == 1)
        g_start = jnp.where(use_top, top_grad, bwd_in)

        def make_bwd(virt_idx):
            acc_pos = 2 * virt_idx

            def run_bwd(operands):
                acc_one = operands[acc_pos]
                acc_two = operands[acc_pos + 1]
                saved_in = lax.dynamic_index_in_dim(act_stash, saved_pos, 0, keepdims=False)
                g_cur = g_start
                for layer_idx in reversed(range(block_len)):
                    g_cur, g_up, g_down = layer_bwd(saved_in[layer_idx], g_cur, up_loc[virt_idx, layer_idx], down_loc[virt_idx, layer_idx])
                    acc_one = add_layer(acc_one, g_up, layer_idx)
                    acc_two = add_layer(acc_two, g_down, layer_idx)
                new_accs = list(operands)
                new_accs[acc_pos] = acc_one
                new_accs[acc_pos + 1] = acc_two
                return tuple(new_accs), g_cur

            return run_bwd

        def skip_bwd(operands):
            return operands, g_start

        branch_list = [skip_bwd, make_bwd(0)] + ([make_bwd(1)] if with_top else [])
        branch_idx = jnp.minimum(jnp.where(b_valid, 1 + b_virt, 0), len(branch_list) - 1)
        acc_list, bwd_out = lax.switch(branch_idx, branch_list, acc_list)

        f_slot = tick_idx - stage_idx
        f_valid = (f_slot >= 0) & (f_slot < 2 * n_micro)
        f_slot = jnp.clip(f_slot, 0, 2 * n_micro - 1)
        f_rem = f_slot % cycle_len
        f_virt = f_rem // n_stage
        f_micro = (f_slot // cycle_len) * n_stage + f_rem % n_stage
        from_data = (stage_idx == 0) & (f_virt == 0)
        h_start = jnp.where(from_data, lax.dynamic_index_in_dim(tokens_loc, f_micro, 0, keepdims=False), fwd_in)
        is_top = (stage_idx == n_stage - 1) & (f_virt == 1)

        def run_fwd(operands):
            stash_cur, loss_cur, top_cur = operands
            w_ones = lax.dynamic_index_in_dim(up_loc, f_virt, 0, keepdims=False)
            w_twos = lax.dynamic_index_in_dim(down_loc, f_virt, 0, keepdims=False)
            h_cur = h_start
            for layer_idx in range(block_len):
                stash_cur = lax.dynamic_update_slice(stash_cur, h_cur[None, None], (f_slot % n_slots, layer_idx, 0, 0))
                h_cur = layer_fwd(h_cur, w_ones[layer_idx], w_twos[layer_idx])
            target_mb = lax.dynamic_index_in_dim(targets_loc, f_micro, 0, keepdims=False)
            out_err = h_cur.astype(jnp.float32) - target_mb.astype(jnp.float32)
            loss_cur = loss_cur + jnp.where(is_top, jnp.sum(out_err * out_err) / (2.0 * n_tok), 0.0)
            top_cur = jnp.where(is_top, (out_err / n_tok).astype(jnp.bfloat16), top_cur)
            return stash_cur, loss_cur, top_cur, h_cur

        def skip_fwd(operands):
            return operands[0], operands[1], operands[2], h_start

        act_stash, loss_acc, top_grad, fwd_out = lax.cond(f_valid, run_fwd, skip_fwd, (act_stash, loss_acc, top_grad))
        fwd_next = lax.ppermute(fwd_out, "stage", fwd_perm)
        bwd_next = lax.ppermute(bwd_out, "stage", bwd_perm)
        return fwd_next, bwd_next, top_grad, act_stash, acc_list, loss_acc

    return tick


def solution(mesh):
    n_stage = mesh.shape["stage"]
    n_data = mesh.shape["data"]

    def device_fn(tokens_loc, targets_loc, up_loc, down_loc):
        n_micro, seq_len, d_model = tokens_loc.shape
        n_tok = n_data * n_micro * seq_len
        block_len = up_loc.shape[1]
        n_slots = min(4 * n_stage, 2 * n_micro)
        zero_act = jnp.zeros((seq_len, d_model), jnp.bfloat16)
        zero_up = jnp.zeros(up_loc.shape[1:], jnp.float32)
        zero_down = jnp.zeros(down_loc.shape[1:], jnp.float32)
        state = (
            zero_act,
            zero_act,
            zero_act,
            jnp.zeros((n_slots, block_len, seq_len, d_model), jnp.bfloat16),
            (zero_up, zero_down, zero_up, zero_down),
            jnp.zeros((), jnp.float32),
        )
        split_tick = 2 * n_micro + 2 * n_stage - 1
        n_ticks = 2 * n_micro + 3 * n_stage - 1
        tick_both = make_tick(n_stage, n_micro, n_tok, tokens_loc, targets_loc, up_loc, down_loc, True)
        fwd_in, bwd_in, top_grad, act_stash, acc_list, loss_acc = lax.fori_loop(0, split_tick, tick_both, state)
        red_up_top = lax.psum_scatter(acc_list[2], "data", scatter_dimension=1, tiled=True)
        red_down_top = lax.psum_scatter(acc_list[3], "data", scatter_dimension=1, tiled=True)
        tick_low = make_tick(n_stage, n_micro, n_tok, tokens_loc, targets_loc, up_loc, down_loc, False)
        state = (fwd_in, bwd_in, top_grad, act_stash, (acc_list[0], acc_list[1]), loss_acc)
        state = lax.fori_loop(split_tick, n_ticks, tick_low, state)
        red_up_low = lax.psum_scatter(state[4][0], "data", scatter_dimension=1, tiled=True)
        red_down_low = lax.psum_scatter(state[4][1], "data", scatter_dimension=1, tiled=True)
        loss = lax.psum(state[5], ("stage", "data"))
        return loss, jnp.stack([red_up_low, red_up_top]), jnp.stack([red_down_low, red_down_top])

    return jax.shard_map(
        device_fn,
        mesh=mesh,
        in_specs=(P("data"), P("data"), P(None, "stage"), P(None, "stage")),
        out_specs=(P(), P(None, "stage", "data"), P(None, "stage", "data")),
        check_vma=False,
    )
```

profile of v0, /device:TPU:0, one launch (start us, length us, event | category | flops | bytes accessed | tf_op | source)
XLA Modules:
  0.0 3001.7 jit_solution(3033451967811267035)
XLA Ops:
  80.9 1291.7 %while.62 = (s32[]{:T(128)}, bf16[512,896]{1,0:T(8,128)(2,1)S(1)}, bf16[512,896]{1,0:T(8,128)(2,1)S(1)}, bf16[512,896]{1,0:T(8,128)(2,1)}, bf16[4,3,512,896]{3,2...) while((s32[]{:T(128)}, bf16[512,896]{1,0:T(8,128)(2,1)S(1)}, ...), condition=%wide.region_7.8_spmd, body=%wide.region_0.7_spmd.sunk | while | flops 94056742912 | bytes 618603200 | solution.py:141
  99.6 80.0 %conditional.8 = ((bf16[4,3,512,896]{3,2,1,0:T(8,128)(2,1)}, f32[]{:T(128)}, bf16[512,896]{1,0:T(8,128)(2,1)}, bf16[512,896]{1,0:T(8,128)(2,1)})) conditional(s32[]{:T(128)} %convert_element_type.575, (bf16[4,3,512,896]{3,2,1,0:T(8,128)(2,1)}, f32[]{:T(128)}, bf16[512,896]{1,0:T(8,128)(2,1)}, bf16[512,896]{1,0:T(8,128)(2,1)}) %tuple.148, ...), branch_computations={%region_1.1_spmd, %region_2.3_spmd} | conditional | flops 26852851712 | bytes 68819792 | solution.py:110
  101.8 20.5 bitcast_dynamic-update-slice_fusion.1
  122.3 26.6 bitcast_dynamic-update-slice_fusion
  148.9 26.9 multiply_reduce_fusion
  179.7 21.8 collective-permute-done
  217.2 80.1 %conditional.8 = ((bf16[4,3,512,896]{3,2,1,0:T(8,128)(2,1)}, f32[]{:T(128)}, bf16[512,896]{1,0:T(8,128)(2,1)}, bf16[512,896]{1,0:T(8,128)(2,1)})) conditional(s32[]{:T(128)} %convert_element_type.575, (bf16[4,3,512,896]{3,2,1,0:T(8,128)(2,1)}, f32[]{:T(128)}, bf16[512,896]{1,0:T(8,128)(2,1)}, bf16[512,896]{1,0:T(8,128)(2,1)}) %tuple.148, ...), branch_computations={%region_1.1_spmd, %region_2.3_spmd} | conditional | flops 26852851712 | bytes 68819792 | solution.py:110
  219.3 20.5 bitcast_dynamic-update-slice_fusion.1
  239.8 26.4 bitcast_dynamic-update-slice_fusion
  266.2 26.9 multiply_reduce_fusion
  299.0 19.2 collective-permute-done
  335.1 79.7 %conditional.8 = ((bf16[4,3,512,896]{3,2,1,0:T(8,128)(2,1)}, f32[]{:T(128)}, bf16[512,896]{1,0:T(8,128)(2,1)}, bf16[512,896]{1,0:T(8,128)(2,1)})) conditional(s32[]{:T(128)} %convert_element_type.575, (bf16[4,3,512,896]{3,2,1,0:T(8,128)(2,1)}, f32[]{:T(128)}, bf16[512,896]{1,0:T(8,128)(2,1)}, bf16[512,896]{1,0:T(8,128)(2,1)}) %tuple.148, ...), branch_computations={%region_1.1_spmd, %region_2.3_spmd} | conditional | flops 26852851712 | bytes 68819792 | solution.py:110
  337.3 20.2 bitcast_dynamic-update-slice_fusion.1
  357.5 26.4 bitcast_dynamic-update-slice_fusion
  383.9 26.9 multiply_reduce_fusion
  415.5 18.8 collective-permute-done
  450.8 79.8 %conditional.8 = ((bf16[4,3,512,896]{3,2,1,0:T(8,128)(2,1)}, f32[]{:T(128)}, bf16[512,896]{1,0:T(8,128)(2,1)}, bf16[512,896]{1,0:T(8,128)(2,1)})) conditional(s32[]{:T(128)} %convert_element_type.575, (bf16[4,3,512,896]{3,2,1,0:T(8,128)(2,1)}, f32[]{:T(128)}, bf16[512,896]{1,0:T(8,128)(2,1)}, bf16[512,896]{1,0:T(8,128)(2,1)}) %tuple.148, ...), branch_computations={%region_1.1_spmd, %region_2.3_spmd} | conditional | flops 26852851712 | bytes 68819792 | solution.py:110
  453.0 20.2 bitcast_dynamic-update-slice_fusion.1
  473.2 26.6 bitcast_dynamic-update-slice_fusion
  499.9 26.8 multiply_reduce_fusion
  564.8 203.0 %collective-permute-start.1 = (bf16[512,896]{1,0:T(8,128)(2,1)S(1)}, bf16[512,896]{1,0:T(8,128)(2,1)S(1)}, u32[]{:S(2)}, u32[]{:S(2)}) collective-permute-start(bf16[512,896]{1,0:T(8,128)(2,1)S(1)} %get-tuple-element.1672), channel_id=1, source_target_pairs={{0,8},{8,0},{1,9},{9,1},{2,10},{10,2},{3,11},{11,3},{4,12},{12,4},... | collective-permute-start | bytes 2752520 | tf_op jit(solution)/shard_map/while/body/eval_jaxpr/ppermute | solution.py:112
  768.9 78.4 %collective-permute-start = (bf16[512,896]{1,0:T(8,128)(2,1)}, bf16[512,896]{1,0:T(8,128)(2,1)S(1)}, u32[]{:S(2)}, u32[]{:S(2)}) collective-permute-start(bf16[512,896]{1,0:T(8,128)(2,1)} %get-tuple-element.1670), channel_id=1, source_target_pairs={{0,8},{8,0},{1,9},{9,1},{2,10},{10,2},{3,11},{11,3},{4,12},{12,4},... | collective-permute-start | bytes 2752520 | tf_op jit(solution)/shard_map/while/body/eval_jaxpr/ppermute | solution.py:111
  866.0 214.9 %conditional.9 = ((f32[3,896,4864]{2,1,0:T(8,128)}, f32[3,4864,896]{2,1,0:T(8,128)}, f32[3,896,4864]{2,1,0:T(8,128)}, f32[3,4864,896]{2,1,0:T(8,128)}, bf16[512,896]{1,0:T(8,128)(2,1)S(1)})) conditional(s32[]{:T(128)} %clamp.27, (f32[3,896,4864]{2,1,0:T(8,128)}, f32[3,4864,896]{2,1,0:T(8,128)}, f32[3,896,4864]{2,1,0:T(8,128)}, ...), branch_computations={%region_4.4_spmd, %region_5.5_spmd, %region_6.6_spmd} | conditional | flops 67202973696 | bytes 536936768 | solution.py:81
  1120.5 214.9 %conditional.9 = ((f32[3,896,4864]{2,1,0:T(8,128)}, f32[3,4864,896]{2,1,0:T(8,128)}, f32[3,896,4864]{2,1,0:T(8,128)}, f32[3,4864,896]{2,1,0:T(8,128)}, bf16[512,896]{1,0:T(8,128)(2,1)S(1)})) conditional(s32[]{:T(128)} %clamp.27, (f32[3,896,4864]{2,1,0:T(8,128)}, f32[3,4864,896]{2,1,0:T(8,128)}, f32[3,896,4864]{2,1,0:T(8,128)}, ...), branch_computations={%region_4.4_spmd, %region_5.5_spmd, %region_6.6_spmd} | conditional | flops 67202973696 | bytes 536936768 | solution.py:81
  1372.5 478.1 %while.63 = (s32[]{:T(128)}, bf16[512,896]{1,0:T(8,128)(2,1)S(1)}, bf16[512,896]{1,0:T(8,128)(2,1)S(1)}, bf16[512,896]{1,0:T(8,128)(2,1)}, bf16[4,3,512,896]{3,2...) while((s32[]{:T(128)}, bf16[512,896]{1,0:T(8,128)(2,1)S(1)}, ...), condition=%wide.region_14.15_spmd, body=%wide.region_8.14_spmd.sunk | while | flops 94056742912 | bytes 578757184 | solution.py:146
  1382.4 196.8 %conditional.11 = ((f32[3,896,4864]{2,1,0:T(8,128)}, f32[3,4864,896]{2,1,0:T(8,128)}, bf16[512,896]{1,0:T(8,128)(2,1)S(1)})) conditional(s32[]{:T(128)} %clamp.28, (f32[3,896,4864]{2,1,0:T(8,128)}, f32[3,4864,896]{2,1,0:T(8,128)}, bf16[512,896]{1,0:T(8,128)(2,1)S(1)}) %tuple.157, (f32[3,896,4864]{2,1,0:T(8,128)}, s32[]{:T(128)}, s32[]{:T(128)}, ...), branch_computations={%region_12.12_spmd, %region_13.13_spmd} | conditional | flops 67202973696 | bytes 497091104 | solution.py:81
  1616.8 196.7 %conditional.11 = ((f32[3,896,4864]{2,1,0:T(8,128)}, f32[3,4864,896]{2,1,0:T(8,128)}, bf16[512,896]{1,0:T(8,128)(2,1)S(1)})) conditional(s32[]{:T(128)} %clamp.28, (f32[3,896,4864]{2,1,0:T(8,128)}, f32[3,4864,896]{2,1,0:T(8,128)}, bf16[512,896]{1,0:T(8,128)(2,1)S(1)}) %tuple.157, (f32[3,896,4864]{2,1,0:T(8,128)}, s32[]{:T(128)}, s32[]{:T(128)}, ...), branch_computations={%region_12.12_spmd, %region_13.13_spmd} | conditional | flops 67202973696 | bytes 497091104 | solution.py:81
  1852.7 32.4 %psum.7 = f32[]{:T(128)} all-reduce(f32[]{:T(128)} %get-tuple-element.1370), channel_id=1, replica_groups=mesh['stage'=2,'data'=8] {'stage','data'}, use_global_device_ids=true, to_apply=%region_15.16 | all-reduce | flops 1 | bytes 8 | tf_op jit(solution)/shard_map/psum | solution.py:149
  1885.1 246.3 %reduce-scatter.9.cloned.1.call-done = f32[3,608,896]{2,1,0:T(8,128)} async-done(((f32[3,4864,896]{2,1,0:T(8,128)}), f32[3,608,896]{2,1,0:T(8,128)}) %reduce-scatter.9.cloned.1.call-update) | async-done | bytes 6537232 | tf_op jit(solution)/shard_map/reduce_scatter | solution.py:148
  2131.4 284.3 %reduce-scatter.11.cloned.1.call-done = f32[3,608,896]{2,1,0:T(8,128)} async-done(((f32[3,4864,896]{2,1,0:T(8,128)}), f32[3,608,896]{2,1,0:T(8,128)}) %reduce-scatter.11.cloned.1.call-update) | async-done | bytes 6537232 | tf_op jit(solution)/shard_map/reduce_scatter | solution.py:143
  2426.2 273.8 %reduce-scatter.5.cloned.1.call-done = f32[3,112,4864]{2,1,0:T(8,128)} async-done(((f32[3,896,4864]{2,1,0:T(8,128)}), f32[3,112,4864]{2,1,0:T(8,128)}) %reduce-scatter.5.cloned.1.call-update) | async-done | bytes 6537232 | tf_op jit(solution)/shard_map/reduce_scatter | solution.py:147
  2700.0 284.1 %reduce-scatter.7.cloned.1.call-done = f32[3,112,4864]{2,1,0:T(8,128)} async-done(((f32[3,896,4864]{2,1,0:T(8,128)}), f32[3,112,4864]{2,1,0:T(8,128)}) %reduce-scatter.7.cloned.1.call-update) | async-done | bytes 6537232 | tf_op jit(solution)/shard_map/reduce_scatter | solution.py:142
  (184 shorter events, 1168.8 us)
Async XLA Ops:
  7.2 2124.2 %reduce-scatter.9.cloned.1.call-start = ((), (), s32[]{:S(2)}) async-start(), calls=%async_computation.6 | async-start | bytes 58834944 | tf_op jit(solution)/shard_map/reduce_scatter | solution.py:148
  96.5 83.3 %collective-permute-start.1 = (bf16[512,896]{1,0:T(8,128)(2,1)S(1)}, bf16[512,896]{1,0:T(8,128)(2,1)S(1)}, u32[]{:S(2)}, u32[]{:S(2)}) collective-permute-start(bf16[512,896]{1,0:T(8,128)(2,1)S(1)} %get-tuple-element.1672), channel_id=1, source_target_pairs={{0,8},{8,0},{1,9},{9,1},{2,10},{10,2},{3,11},{11,3},{4,12},{12,4},... | collective-permute-start | bytes 2752520 | tf_op jit(solution)/shard_map/while/body/eval_jaxpr/ppermute | solution.py:112
  179.7 21.8 collective-permute-start
  217.0 82.1 %collective-permute-start.1 = (bf16[512,896]{1,0:T(8,128)(2,1)S(1)}, bf16[512,896]{1,0:T(8,128)(2,1)S(1)}, u32[]{:S(2)}, u32[]{:S(2)}) collective-permute-start(bf16[512,896]{1,0:T(8,128)(2,1)S(1)} %get-tuple-element.1672), channel_id=1, source_target_pairs={{0,8},{8,0},{1,9},{9,1},{2,10},{10,2},{3,11},{11,3},{4,12},{12,4},... | collective-permute-start | bytes 2752520 | tf_op jit(solution)/shard_map/while/body/eval_jaxpr/ppermute | solution.py:112
  297.3 21.0 collective-permute-start
  333.6 81.9 %collective-permute-start.1 = (bf16[512,896]{1,0:T(8,128)(2,1)S(1)}, bf16[512,896]{1,0:T(8,128)(2,1)S(1)}, u32[]{:S(2)}, u32[]{:S(2)}) collective-permute-start(bf16[512,896]{1,0:T(8,128)(2,1)S(1)} %get-tuple-element.1672), channel_id=1, source_target_pairs={{0,8},{8,0},{1,9},{9,1},{2,10},{10,2},{3,11},{11,3},{4,12},{12,4},... | collective-permute-start | bytes 2752520 | tf_op jit(solution)/shard_map/while/body/eval_jaxpr/ppermute | solution.py:112
  414.7 19.6 collective-permute-start
  449.7 81.6 %collective-permute-start.1 = (bf16[512,896]{1,0:T(8,128)(2,1)S(1)}, bf16[512,896]{1,0:T(8,128)(2,1)S(1)}, u32[]{:S(2)}, u32[]{:S(2)}) collective-permute-start(bf16[512,896]{1,0:T(8,128)(2,1)S(1)} %get-tuple-element.1672), channel_id=1, source_target_pairs={{0,8},{8,0},{1,9},{9,1},{2,10},{10,2},{3,11},{11,3},{4,12},{12,4},... | collective-permute-start | bytes 2752520 | tf_op jit(solution)/shard_map/while/body/eval_jaxpr/ppermute | solution.py:112
  530.6 18.7 collective-permute-start
  564.8 282.5 %collective-permute-start.1 = (bf16[512,896]{1,0:T(8,128)(2,1)S(1)}, bf16[512,896]{1,0:T(8,128)(2,1)S(1)}, u32[]{:S(2)}, u32[]{:S(2)}) collective-permute-start(bf16[512,896]{1,0:T(8,128)(2,1)S(1)} %get-tuple-element.1672), channel_id=1, source_target_pairs={{0,8},{8,0},{1,9},{9,1},{2,10},{10,2},{3,11},{11,3},{4,12},{12,4},... | collective-permute-start | bytes 2752520 | tf_op jit(solution)/shard_map/while/body/eval_jaxpr/ppermute | solution.py:112
  768.9 94.2 %collective-permute-start = (bf16[512,896]{1,0:T(8,128)(2,1)}, bf16[512,896]{1,0:T(8,128)(2,1)S(1)}, u32[]{:S(2)}, u32[]{:S(2)}) collective-permute-start(bf16[512,896]{1,0:T(8,128)(2,1)} %get-tuple-element.1670), channel_id=1, source_target_pairs={{0,8},{8,0},{1,9},{9,1},{2,10},{10,2},{3,11},{11,3},{4,12},{12,4},... | collective-permute-start | bytes 2752520 | tf_op jit(solution)/shard_map/while/body/eval_jaxpr/ppermute | solution.py:111
  911.3 43.4 %copy-start.9 = (bf16[512,896]{1,0:T(8,128)(2,1)}, bf16[512,896]{1,0:T(8,128)(2,1)S(1)}, u32[]{:S(2)}) copy-start(bf16[512,896]{1,0:T(8,128)(2,1)S(1)} %add_convert_fusion.8) | copy-start | bytes 2752516 | tf_op jit(solution)/shard_map/while/body/eval_jaxpr/cond
  978.9 27.6 slice-start.2
  990.5 16.1 slice-start.3
  1080.9 23.3 collective-permute-start.1
  1088.3 29.3 collective-permute-start
  1165.8 43.4 %copy-start.9 = (bf16[512,896]{1,0:T(8,128)(2,1)}, bf16[512,896]{1,0:T(8,128)(2,1)S(1)}, u32[]{:S(2)}) copy-start(bf16[512,896]{1,0:T(8,128)(2,1)S(1)} %add_convert_fusion.8) | copy-start | bytes 2752516 | tf_op jit(solution)/shard_map/while/body/eval_jaxpr/cond
  1233.5 27.6 slice-start.2
  1245.0 16.1 slice-start.3
  1335.4 23.3 collective-permute-start.1
  1342.8 28.4 collective-permute-start
  1434.0 27.6 copy-start.10
  1485.9 27.6 slice-start.4
  1579.1 23.3 collective-permute-start.3
  1586.5 27.6 collective-permute-start.2
  1668.7 27.6 copy-start.10
  1720.3 27.6 slice-start.4
  1813.6 23.3 collective-permute-start.3
  1821.0 26.7 collective-permute-start.2
  1850.6 565.0 %reduce-scatter.11.cloned.1.call-start = ((), (), s32[]{:S(2)}) async-start(), calls=%async_computation.7 | async-start | bytes 58834944 | tf_op jit(solution)/shard_map/reduce_scatter | solution.py:143
  1851.4 848.6 %reduce-scatter.5.cloned.1.call-start = ((), (), s32[]{:S(2)}) async-start(), calls=%async_computation.4 | async-start | bytes 58834944 | tf_op jit(solution)/shard_map/reduce_scatter | solution.py:147
  1852.1 1132.0 %reduce-scatter.7.cloned.1.call-start = ((), (), s32[]{:S(2)}) async-start(), calls=%async_computation.5 | async-start | bytes 58834944 | tf_op jit(solution)/shard_map/reduce_scatter | solution.py:142
  (12 other events, 131.2 us)
Sparse Core Ops, SparseCore 0:
  1850.8 280.5 reduce-scatter.8
  2135.1 280.5 reduce-scatter.10
  2419.4 280.5 reduce-scatter.4
  2703.5 280.5 reduce-scatter.6
where the time goes:
time: 3010 us; the launch traced here: 3000 us
  waiting for transfers between devices  1290 us (43%)
  matrix products  1070 us (36%)
  starting transfers between devices  295 us (10%)
  loops' own time  153 us (5%)
  local copies, waits for them, and re-layouts  87.1 us (3%)
  other arithmetic  54.4 us (2%)
  blocking collectives  32.4 us (1%)
    dot_general x12, matrix products, layer_fwd(): jnp.dot(act_bf, w_two, preferred_element_type=jnp.float32)  295 us
    reduce_scatter x1, waiting for transfers between devices, device_fn(): lax.psum_scatter(acc_list[3], 'data', scatter_dimension=1, tiled=True)  284 us
    reduce_scatter x1, waiting for transfers between devices, device_fn(): lax.psum_scatter(acc_list[2], 'data', scatter_dimension=1, tiled=True)  284 us
    reduce_scatter x1, waiting for transfers between devices, device_fn(): lax.psum_scatter(state[4][0], 'data', scatter_dimension=1, tiled=True)  274 us
    reduce_scatter x1, waiting for transfers between devices, device_fn(): lax.psum_scatter(state[4][1], 'data', scatter_dimension=1, tiled=True)  246 us
    ppermute x9, starting transfers between devices, tick(): bwd_next = lax.ppermute(bwd_out, 'stage', bwd_perm)  211 us
    dot_general x12, matrix products, layer_bwd(): jnp.einsum('tf,td->fd', act_bf, grad_out, preferred_element_type=jnp.floa...  191 us
    dot_general x12, matrix products, layer_bwd(): jnp.einsum('td,tf->df', h_in, d_pre, preferred_element_type=jnp.float32)  172 us
  transfers between devices with their start and end apart: 22, of which 17 were waited for; matrix products, arithmetic and copies ran while one was open for 11% of the time, Pallas kernels for 0%

commit v1 on v0

v1 whole, which is shorter than its diff:
```python
import jax
import jax.numpy as jnp
import numpy as np
from jax import lax
from jax.experimental import pallas as pl
from jax.experimental.pallas import tpu as pltpu
from jax.sharding import PartitionSpec as P

F32, BF16 = jnp.float32, jnp.bfloat16
MESH = pl.DeviceIdType.MESH
N_CHUNK = 4
N_LAYER = 3
HALF = 2 * N_CHUNK
N_TILE = 2 * HALF * N_LAYER
N_GRAD = 2 * N_LAYER
N_STEP = 8
LONG, SHORT = 8 * N_LAYER, 4 * N_LAYER
NT = (((1,), (1,)), ((), ()))
TN = (((0,), (0,)), ((), ()))
C0 = 0.7978845608028654
C1 = 0.044715
ANY = pl.BlockSpec(memory_space=pl.ANY)


def gelu(z):
    return z * (0.5 * (1.0 + jnp.tanh(C0 * (z + C1 * (z * z * z)))))


def gelu_and_slope(z):
    z2 = z * z
    t = jnp.tanh(C0 * (z + C1 * (z2 * z)))
    cdf = 0.5 * (1.0 + t)
    slope = cdf + (0.5 * z) * ((1.0 - t * t) * (C0 + (3.0 * C0 * C1) * z2))
    return cdf * z, slope


def sub_blocks(ff):
    step = 1280
    return [(o, min(step, ff - o)) for o in range(0, ff, step)]


def window_width(ff):
    return (ff // 4 + 127) // 128 * 128


class Place:
    def __init__(self, stage, dev):
        self.stage, self.dev = stage, dev
        self.y, self.x, self.c = dev // 4, (dev // 2) % 2, dev % 2

    def flip(self, fy, fx, fc):
        return self.dev + fy * (4 - 8 * self.y) + fx * (2 - 4 * self.x) + fc * (1 - 2 * self.c)

    def gather(self, v, k):
        is_y = (v + k) % 2
        kind_c = (1 - v) * (1 - k // 2)
        one = self.flip(is_y, 1 - is_y, 0)
        two = self.flip(kind_c * (1 - is_y), kind_c * is_y, 1 - kind_c)
        return one, two

    def layer(self, j):
        return 1 - j // N_LAYER, N_LAYER - 1 - j % N_LAYER

    def share(self, j):
        y, x, c = self.y, self.x, self.c
        v, k = self.layer(j)
        kc = j // 4
        dy = (1 - kc) * ((v + k) % 2)
        dx = (1 - kc) * (1 - (v + k) % 2)
        sh = Share()
        sh.kc = kc
        sh.p = (dy + kc) * y + dx * c
        sh.q = dy * c + (dx + kc) * x
        sh.wu, sh.w1, sh.w2 = 2 * dy + 4 * dx + kc, 4 * dy + 2 * dx + 4 * kc, dy + dx + 2 * kc
        sh.u = dy * x + dx * y + kc * c
        sh.r1 = dy * y + dx * x + kc * y
        sh.r2 = (dy + dx) * c + kc * x
        sh.partner = self.dev + sh.wu * (1 - 2 * sh.u)
        away = (1 - kc) * (sh.u * (1 - c) + c * (1 - sh.u))
        sh.away = away
        sh.dest_same = self.dev + away * sh.wu * (1 - 2 * sh.u)
        sh.dest_other = sh.dest_same + (1 - 2 * c)
        sh.slot_other = kc + away
        return sh


class Share:
    def piece(self, i):
        r1 = self.r1 + (i // 2) * (1 - 2 * self.r1)
        r2 = self.r2 + (i % 2) * (1 - 2 * self.r2)
        return self.w1 * r1 + self.w2 * r2 + self.wu * self.u

    def start(self, ff):
        return (ff // 2) * self.p + (ff // 2 - window_width(ff)) * self.q

    def base(self, ff):
        return (ff // 4 - (ff // 2 - window_width(ff))) * self.q


def layer_of(s):
    e = s // N_LAYER
    r = s - N_LAYER * e
    back = e // HALF
    return e, r + back * (N_LAYER - 1 - 2 * r)


def block_of(e):
    back = e // HALF
    first = (e - HALF * back) // N_CHUNK
    return first + back * (1 - 2 * first)


def step_kernel(n_tok, tokens, targets, wu, wd, hg, dd, upp, loss_ref, sup, kup, ub, sd, zin, lbuf, sems):
    place = Place(lax.axis_index("stage"), lax.axis_index("data"))
    stage, dev, c = place.stage, place.dev, place.c
    d, ff = wu.shape[2:]
    rows = zin.shape[1]
    tile = (rows, d)

    def remote(src, dst, send, recv, to):
        return pltpu.make_async_remote_copy(src, dst, send, recv, to, MESH)

    def at(index):
        return (stage, index)

    z_peer = (1 - stage, dev)
    local_peers = [place.flip(*f) for f in ((0, 0, 1), (0, 1, 0), (1, 0, 0), (0, 1, 1), (1, 0, 1), (1, 1, 0))]

    @pl.when(stage == 0)
    def _():
        for m in range(N_CHUNK):
            pltpu.make_async_copy(tokens.at[m], zin.at[m], sems.z_recv.at[m]).start()

    barrier = pltpu.get_barrier_semaphore()
    for peer in [z_peer] + [at(i) for i in local_peers]:
        pl.semaphore_signal(barrier, inc=1, device_id=peer, device_id_type=MESH)
    pl.semaphore_wait(barrier, 1 + len(local_peers))

    def a_copy(s):
        e, l = layer_of(s)
        one, _ = place.gather(block_of(e), l)
        return remote(hg.at[0, e, l], hg.at[1, e, l], sems.a_send, sems.a_recv.at[s], at(one))

    def c_copy(s):
        e, l = layer_of(s)
        v = block_of(e)
        _, two = place.gather(v, l)
        return remote(hg.at[0, e, l], hg.at[2, e, l], sems.c_send, sems.c_recv.at[v], at(two))

    def forward(s):
        e, l = layer_of(s)
        v = block_of(e)
        _, two = place.gather(v, l)
        a_copy(s).wait_recv()
        remote(hg.at[1, e, l], hg.at[3, e, l], sems.f_send, sems.f_recv.at[v], at(two)).start()

    def chain(wub, wdb, ring, zout, hld, tgt, acc, loss_row):
        subs = sub_blocks(ff)

        def weight_copies(v, l):
            return (
                pltpu.make_async_copy(wu.at[v, l], wub.at[l], sems.w.at[l, 0]),
                pltpu.make_async_copy(wd.at[v, l], wdb.at[l], sems.w.at[l, 1]),
            )

        def load_weights(v, l):
            for cp in weight_copies(v, l):
                cp.start()

        def wait_weights(l):
            for cp in weight_copies(0, l):
                cp.wait()

        def z_copy(m):
            return remote(zout, zin.at[m], sems.z_send, sems.z_recv.at[m], z_peer)

        def sent(e):
            fwd = (e < HALF) & ((stage == 0) | (e < N_CHUNK))
            return fwd | ((e >= HALF) & ((stage == 1) | (e < HALF + N_CHUNK)))

        def start_tile(s, e, l, first):
            @pl.when(first)
            def _():
                @pl.when(jnp.logical_not((stage == 1) & (e >= HALF) & (e < HALF + N_CHUNK)))
                def _():
                    z_copy(e % N_CHUNK).wait_recv()

                ring[s % 3] = zin[e % N_CHUNK]

            pltpu.make_async_copy(ring.at[s % 3], hg.at[0, e, l], sems.ld).start()

        def end_tile(s, e, l, last):
            pltpu.make_async_copy(ring.at[s % 3], hg.at[0, e, l], sems.ld).wait()
            a_copy(s).start()
            c_copy(s).start()

            @pl.when((s >= LONG) & (s < 2 * LONG))
            def _():
                forward(s - LONG)

            @pl.when(s >= LONG + SHORT)
            def _():
                forward(s - SHORT)

            @pl.when(last & (e >= 1))
            def _():
                @pl.when(sent(e - 1))
                def _():
                    z_copy(0).wait_send()

        for l in range(N_LAYER):
            load_weights(0, l)
        loss_row[...] = jnp.zeros_like(loss_row)

        def fwd_step(s, _):
            e, l = layer_of(s)
            v, m = e // N_CHUNK, e % N_CHUNK
            top = (stage == 1) & (v == 1)
            start_tile(s, e, l, l == 0)

            @pl.when(top & (l == 0))
            def _():
                pltpu.make_async_copy(targets.at[m], tgt, sems.t).start()

            @pl.when(m == 0)
            def _():
                wait_weights(l)

            for i, (off, w) in enumerate(subs):
                h = ring[s % 3]
                z = jnp.dot(h, wub[l, :, off : off + w], preferred_element_type=F32)
                a = gelu(z).astype(BF16)
                part = jnp.dot(a, wdb[l, off : off + w, :], preferred_element_type=F32)
                acc[...] = (h.astype(F32) if i == 0 else acc[...]) + part

            end_tile(s, e, l, l == N_LAYER - 1)

            @pl.when(e == N_CHUNK - 1)
            def _():
                load_weights(1, l)

            @pl.when(l < N_LAYER - 1)
            def _():
                ring[(s + 1) % 3] = acc[...].astype(BF16)

            @pl.when(l == N_LAYER - 1)
            def _():
                @pl.when(top)
                def _():
                    pltpu.make_async_copy(targets.at[m], tgt, sems.t).wait()
                    err = acc[...].astype(BF16).astype(F32) - tgt[...].astype(F32)
                    loss_row[...] += jnp.sum(err * err, axis=0, keepdims=True)
                    zin[m] = (err * (1.0 / n_tok)).astype(BF16)

                @pl.when(jnp.logical_not(top))
                def _():
                    zout[...] = acc[...].astype(BF16)

                @pl.when(sent(e))
                def _():
                    z_copy(m).start()

            return 0

        lax.fori_loop(0, N_TILE // 2, fwd_step, 0)

        def h_copy(s):
            e, l = layer_of(s)
            src = N_CHUNK * block_of(e) + e % N_CHUNK
            return pltpu.make_async_copy(hg.at[0, src, l], hld.at[s % 2], sems.h.at[s % 2])

        h_copy(N_TILE // 2).start()

        def bwd_step(s, _):
            e, l = layer_of(s)
            m = e % N_CHUNK

            @pl.when(s + 1 < N_TILE)
            def _():
                h_copy(s + 1).start()

            start_tile(s, e, l, l == N_LAYER - 1)
            h_copy(s).wait()

            @pl.when(e == HALF + N_CHUNK)
            def _():
                wait_weights(l)

            for i, (off, w) in enumerate(subs):
                g = ring[s % 3]
                z = jnp.dot(hld[s % 2], wub[l, :, off : off + w], preferred_element_type=F32)
                da = lax.dot_general(g, wdb[l, off : off + w, :], NT, preferred_element_type=F32)
                _, slope = gelu_and_slope(z)
                dz = (slope * da.astype(BF16).astype(F32)).astype(BF16)
                part = lax.dot_general(dz, wub[l, :, off : off + w], NT, preferred_element_type=F32)
                acc[...] = (g.astype(F32) if i == 0 else acc[...]) + part

            end_tile(s, e, l, l == 0)

            @pl.when(e == HALF + N_CHUNK - 1)
            def _():
                load_weights(0, l)

            @pl.when(l > 0)
            def _():
                ring[(s + 1) % 3] = acc[...].astype(BF16)

            @pl.when(l == 0)
            def _():
                zout[...] = acc[...].astype(BF16)

                @pl.when(sent(e))
                def _():
                    z_copy(m).start()

            return 0

        lax.fori_loop(N_TILE // 2, N_TILE, bwd_step, 0)

        @pl.when(sent(2 * HALF - 1))
        def _():
            z_copy(0).wait_send()

        loss_ref[...] = jnp.broadcast_to(jnp.sum(loss_row[...], axis=1, keepdims=True), loss_ref.shape)

    width = window_width(ff)
    seg_d, seg_u = dd.shape[2], upp.shape[2]

    def grads(wub, wdb, hb, gb, gd, gu, cb, ubb):
        def weight_copies(j):
            v, k = place.layer(j)
            start = pl.multiple_of(place.share(j).start(ff), 128)
            b = j % 2
            return (
                pltpu.make_async_copy(wu.at[v, k, :, pl.ds(start, width)], wub.at[b], sems.ww.at[b, 0]),
                pltpu.make_async_copy(wd.at[v, k, pl.ds(start, width), :], wdb.at[b], sems.ww.at[b, 1]),
            )

        def fetches(n):
            v, k = place.layer(n // N_STEP)
            t = n % N_STEP
            m, part = t // 2, 2 * (t % 2)
            h_at = N_CHUNK * v + part
            g_at = HALF + N_CHUNK * (1 - v) + part
            b = n % 2
            return (
                pltpu.make_async_copy(hg.at[m, pl.ds(h_at, 2), k], hb.at[b], sems.hb.at[b]),
                pltpu.make_async_copy(hg.at[m, pl.ds(g_at, 2), k], gb.at[b], sems.gb.at[b]),
            )

        def arrived(v):
            ref = hg.at[2, pl.ds(0, HALF)]
            remote(ref, ref, sems.c_send, sems.c_recv.at[v], z_peer).wait_recv()
            remote(ref, ref, sems.f_send, sems.f_recv.at[v], z_peer).wait_recv()

        def stage_copies(j):
            sh = place.share(j)
            b = j % 2
            up = []
            for i in range(4):
                keep = sh.piece(i)
                send = keep + sh.wu * (1 - 2 * sh.u)
                for to, row, sem in ((sup, send, 0), (kup, keep, 1)):
                    src = gu.at[b, pl.ds(pl.multiple_of(row * seg_u, 8), seg_u), :]
                    up.append(pltpu.make_async_copy(src, to.at[j, i], sems.st.at[sem]))
            base = sh.base(ff)
            part = [gd.at[b, pl.ds(pl.multiple_of(base + seg_d * i, 8), seg_d), :] for i in (c, 1 - c)]
            same = [pltpu.make_async_copy(part[0], to.at[j, 0], sems.st.at[2]) for to in (dd, sd)]
            other = pltpu.make_async_copy(part[1], sd.at[j, 1], sems.st.at[3])
            return sh, up, same, other

        def stage_out(j):
            sh, up, same, other = stage_copies(j)
            for cp in up:
                cp.start()
            other.start()
            pl.when(sh.away == 0)(same[0].start)
            pl.when(sh.away == 1)(same[1].start)

        def down_same(j, sh):
            return remote(sd.at[j, 0], dd.at[j, 1], sems.ds_send, sems.d_recv.at[j, 1], at(sh.dest_same))

        def up_exchange(j, sh):
            return remote(sup.at[j], ub.at[j], sems.u_send, sems.u_recv.at[j], at(sh.partner))

        def send_out(j):
            sh = place.share(j)
            pltpu.make_async_copy(sup.at[j], sup.at[j], sems.st.at[0]).wait()
            up_exchange(j, sh).start()
            pltpu.make_async_copy(sd.at[j, 1], sd.at[j, 1], sems.st.at[3]).wait()
            slot = sh.slot_other
            remote(
                sd.at[j, 1], dd.at[j, slot], sems.d_send, sems.d_recv.at[j, slot], at(sh.dest_other)
            ).start()

            pltpu.make_async_copy(sd.at[j, 0], sd.at[j, 0], sems.st.at[2]).wait()
            pl.when(sh.away == 1)(down_same(j, sh).start)
            pltpu.make_async_copy(kup.at[j], kup.at[j], sems.st.at[1]).wait()

        def piece_sends(j, b):
            sh = place.share(j)
            out = [pltpu.make_async_copy(cb.at[b, 0], upp.at[j, 0], sems.p_here.at[b])]
            for i in range(1, 4):
                out.append(remote(cb.at[b, i], upp.at[j, i], sems.p_send.at[b], sems.p_recv.at[j], at(sh.piece(i))))
            return out

        def wait_pieces(j, b):
            piece_sends(j, b)[0].wait()
            ref = cb.at[b, pl.ds(1, 3)]
            remote(ref, ref, sems.p_send.at[b], sems.p_recv.at[j], z_peer).wait_send()

        def sum_loads(j, b):
            return (
                pltpu.make_async_copy(kup.at[j], cb.at[b], sems.cl.at[0]),
                pltpu.make_async_copy(ub.at[j], ubb, sems.cl.at[1]),
            )

        def sum_load(j, b):
            up_exchange(j, place.share(j)).wait_recv()
            for cp in sum_loads(j, b):
                cp.start()

        def sum_add(j, b):
            for cp in sum_loads(j, b):
                cp.wait()
            cb[b] += ubb[...]
            for cp in piece_sends(j, b):
                cp.start()

        for cp in weight_copies(0) + fetches(0):
            cp.start()

        loss_peers = [at(place.flip(0, 0, 1)), at(place.flip(0, 1, 0)), at(place.flip(1, 0, 0)), z_peer]

        def loss_copy(r):
            return remote(lbuf.at[0, r], lbuf.at[1, r], sems.l_send, sems.l_recv.at[r], loss_peers[r])

        def step(n, _):
            j, t = n // N_STEP, n % N_STEP
            b, jb = n % 2, j % 2

            @pl.when((n >= SHORT) & (n < 2 * SHORT))
            def _():
                forward(n + LONG)

            for v, when in ((1, 3), (0, N_LAYER * N_STEP + 3)):
                pl.when(n == when)(lambda v=v: arrived(v))

            @pl.when(n + 1 < N_GRAD * N_STEP)
            def _():
                for cp in fetches(n + 1):
                    cp.start()

            for r in range(4):

                @pl.when(n == 2 * r)
                def _():
                    if r:
                        loss_copy(r - 1).wait()
                        loss_ref[...] += lbuf[1, r - 1]
                    lbuf[0, r] = loss_ref[...]

                @pl.when(n == 2 * r + 1)
                def _():
                    loss_copy(r).start()

            @pl.when(n == 8)
            def _():
                loss_copy(3).wait()
                loss_ref[...] += lbuf[1, 3]

            @pl.when(t == 0)
            def _():
                for cp in weight_copies(j):
                    cp.wait()

            @pl.when((t == 1) & (j + 1 < N_GRAD))
            def _():
                for cp in weight_copies(j + 1):
                    cp.start()

            @pl.when((t == 0) & (j >= 1))
            def _():
                stage_out(j - 1)

            @pl.when((t == 1) & (j >= 1))
            def _():
                send_out(j - 1)

            @pl.when((t == 4) & (j >= 3))
            def _():
                @pl.when(j == 5)
                def _():
                    wait_pieces(0, 0)

                sum_load(j - 3, (j - 3) % 2)

            @pl.when((t == 5) & (j >= 3))
            def _():
                sum_add(j - 3, (j - 3) % 2)

            @pl.when(n == N_GRAD * N_STEP - 2)
            def _():
                wait_pieces(1, 1)
                sum_load(4, 1)

            @pl.when(n == N_GRAD * N_STEP - 1)
            def _():
                sum_add(4, 1)

            for cp in fetches(n):
                cp.wait()
            h = hb[b].reshape(2 * rows, d)
            g = gb[b].reshape(2 * rows, d)
            z = jnp.dot(h, wub[jb], preferred_element_type=F32)
            da = lax.dot_general(g, wdb[jb], NT, preferred_element_type=F32).astype(BF16).astype(F32)
            a, slope = gelu_and_slope(z)
            a = a.astype(BF16)
            dz = (slope * da).astype(BF16)
            gd[jb] = jnp.where(t == 0, 0.0, gd[jb]) + lax.dot_general(a, g, TN, preferred_element_type=F32)
            gu[jb] = jnp.where(t == 0, 0.0, gu[jb]) + lax.dot_general(h, dz, TN, preferred_element_type=F32)
            return 0

        lax.fori_loop(0, N_GRAD * N_STEP, step, 0)
        stage_out(5)
        send_out(5)
        wait_pieces(4, 1)
        sum_load(5, 1)
        sum_add(5, 1)
        wait_pieces(2, 0)
        sum_load(3, 0)
        sum_add(3, 0)
        wait_pieces(5, 1)
        wait_pieces(3, 0)

    pl.run_scoped(
        chain,
        pltpu.VMEM((N_LAYER, d, ff), BF16),
        pltpu.VMEM((N_LAYER, ff, d), BF16),
        pltpu.VMEM((3, *tile), BF16),
        pltpu.VMEM(tile, BF16),
        pltpu.VMEM((2, *tile), BF16),
        pltpu.VMEM(tile, BF16),
        pltpu.VMEM(tile, F32),
        pltpu.VMEM((1, d), F32),
    )
    pl.run_scoped(
        grads,
        pltpu.VMEM((2, d, width), BF16),
        pltpu.VMEM((2, width, d), BF16),
        pltpu.VMEM((2, 2, *tile), BF16),
        pltpu.VMEM((2, 2, *tile), BF16),
        pltpu.VMEM((2, width, d), F32),
        pltpu.VMEM((2, d, width), F32),
        pltpu.VMEM((2, 4, seg_u, width), F32),
        pltpu.VMEM((4, seg_u, width), F32),
    )

    for j in range(N_GRAD):
        sh = place.share(j)
        ref = upp.at[j, pl.ds(1, 3)]
        remote(ref, ref, sems.p_send.at[0], sems.p_recv.at[j], z_peer).wait_recv()
        ref = dd.at[j, 0]
        remote(ref, ref, sems.d_send, sems.d_recv.at[j, 1], z_peer).wait_recv()

        @pl.when(sh.away == 1)
        def _():
            remote(ref, ref, sems.ds_send, sems.d_recv.at[j, 0], z_peer).wait()

    remote(sup, sup, sems.u_send, sems.u_recv.at[0], z_peer).wait_send()
    ref = sd.at[:, 1]
    remote(ref, ref, sems.d_send, sems.d_recv.at[0, 0], z_peer).wait_send()
    for sem in (sems.a_send, sems.c_send, sems.f_send):
        remote(hg.at[0], hg.at[0], sem, sems.a_recv.at[0], z_peer).wait_send()


SEMS = {
    "w": (N_LAYER, 2),
    "ld": (),
    "h": (2,),
    "t": (),
    "z_send": (),
    "z_recv": (N_CHUNK,),
    "a_send": (),
    "a_recv": (N_TILE,),
    "c_send": (),
    "c_recv": (2,),
    "f_send": (),
    "f_recv": (2,),
    "ww": (2, 2),
    "hb": (2,),
    "gb": (2,),
    "st": (4,),
    "u_send": (),
    "u_recv": (N_GRAD,),
    "d_send": (),
    "ds_send": (),
    "d_recv": (N_GRAD, 2),
    "cl": (2,),
    "p_send": (2,),
    "p_here": (2,),
    "p_recv": (N_GRAD,),
    "l_send": (),
    "l_recv": (4,),
}


class Sems:
    def __init__(self, refs):
        for name, ref in zip(SEMS, refs, strict=True):
            setattr(self, name, ref)


def step_call(tokens, targets, wu, wd, n_tok, n_data):
    n_chunk, rows, d = tokens.shape
    ff = wu.shape[-1]
    width = window_width(ff)
    pieces = jax.ShapeDtypeStruct((N_GRAD, 4, d // n_data, width), F32)
    parts = jax.ShapeDtypeStruct((N_GRAD, 2, ff // n_data, d), F32)

    def body(*refs):
        n = 12 + 2
        step_kernel(n_tok, *refs[:n], Sems(refs[n:]))

    return pl.pallas_call(
        body,
        in_specs=[ANY] * 4,
        out_specs=[ANY] * 3 + [pl.BlockSpec(memory_space=pltpu.VMEM)] + [ANY] * 4,
        out_shape=[
            jax.ShapeDtypeStruct((4, 2 * HALF, N_LAYER, rows, d), BF16),
            parts,
            pieces,
            jax.ShapeDtypeStruct((8, 128), F32),
            pieces,
            pieces,
            pieces,
            parts,
        ],
        scratch_shapes=[
            pltpu.VMEM((n_chunk, rows, d), BF16),
            pltpu.VMEM((2, 4, 8, 128), F32),
            *[pltpu.SemaphoreType.DMA(shape) for shape in SEMS.values()],
        ],
        compiler_params=pltpu.CompilerParams(collective_id=0, has_side_effects=True, vmem_limit_bytes=67043328),
        name="step",
    )(tokens, targets, wu, wd)


def final_kernel(scal, dd, upp, down_ref, up_ref):
    down_ref[0, 0] = dd[0, 0] + dd[0, 1]
    width = upp.shape[-1]
    for i in range(4):
        start = pl.multiple_of(scal[4 * pl.program_id(0) + i], 128)
        up_ref[0, 0, :, pl.ds(start, width)] = upp[0, i]


def final_call(scal, dd, upp, n_data):
    seg_d, d = dd.shape[2:]
    seg_u, width = upp.shape[2:]
    ff = seg_d * n_data
    return pl.pallas_call(
        final_kernel,
        grid_spec=pltpu.PrefetchScalarGridSpec(
            num_scalar_prefetch=1,
            grid=(N_GRAD,),
            in_specs=[
                pl.BlockSpec((1, 2, seg_d, d), lambda j, s: (j, 0, 0, 0)),
                pl.BlockSpec((1, 4, seg_u, width), lambda j, s: (j, 0, 0, 0)),
            ],
            out_specs=[
                pl.BlockSpec((1, 1, seg_d, d), lambda j, s: (1 - j // N_LAYER, N_LAYER - 1 - j % N_LAYER, 0, 0)),
                pl.BlockSpec((1, 1, seg_u, ff), lambda j, s: (1 - j // N_LAYER, N_LAYER - 1 - j % N_LAYER, 0, 0)),
            ],
        ),
        out_shape=[
            jax.ShapeDtypeStruct((2, N_LAYER, seg_d, d), F32),
            jax.ShapeDtypeStruct((2, N_LAYER, seg_u, ff), F32),
        ],
        compiler_params=pltpu.CompilerParams(dimension_semantics=("arbitrary",), vmem_limit_bytes=40 * 2**20),
        name="final",
    )(scal, dd, upp)


def window_table(n_data, ff):
    table = []
    for dev in range(n_data):
        place = Place(0, dev)
        row = []
        for j in range(N_GRAD):
            for i in range(4):
                row.append(Place(0, place.share(j).piece(i)).share(j).start(ff))
        table.append(row)
    return np.array(table, np.int32)


def solution(mesh):
    n_data = mesh.shape["data"]

    def device_fn(tokens_loc, targets_loc, wu, wd):
        n_micro, seq_len, d = tokens_loc.shape
        n_tok = n_data * n_micro * seq_len
        ff = wu.shape[-1]
        rows = n_micro * seq_len // N_CHUNK
        tokens = tokens_loc.reshape(N_CHUNK, rows, d)
        targets = targets_loc.reshape(N_CHUNK, rows, d)
        out = step_call(tokens, targets, wu, wd, n_tok, n_data)
        dd, upp, loss = out[1:4]
        starts = jnp.asarray(window_table(n_data, ff))
        scal = lax.dynamic_index_in_dim(starts, lax.axis_index("data"), 0, keepdims=False)
        down, up = final_call(scal, dd, upp, n_data)
        return loss[0, 0] / (2.0 * n_tok), up, down

    return jax.shard_map(
        device_fn,
        mesh=mesh,
        in_specs=(P("data"), P("data"), P(None, "stage"), P(None, "stage")),
        out_specs=(P(), P(None, "stage", "data"), P(None, "stage", "data")),
        check_vma=False,
    )
```

time: 3010 us -> 903 us (0.30)
  waiting for transfers between devices: 1290 us -> 0 us
  matrix products: 1070 us -> 0 us
  Pallas kernels: 0 us -> 892 us
  starting transfers between devices: 295 us -> 0 us
  loops' own time: 153 us -> 0 us
  local copies, waits for them, and re-layouts: 87.1 us -> 6.79 us
  other arithmetic: 54.4 us -> 0 us
  blocking collectives: 32.4 us -> 0 us
    reduce_scatter x4 -> x0, waiting for transfers between devices: 1090 us -> none  [the longest x1 284 us: device_fn(): lax.psum_scatter(acc_list[3], 'data', scatter_dimension=1, tiled=True)]
    dot_general x72 -> x0, matrix products: 1070 us -> none  [the longest x12 295 us: layer_fwd(): jnp.dot(act_bf, w_two, preferred_element_type=jnp.float32)]
    pallas_call x0 -> x2, Pallas kernels: none -> 892 us  [the longest x1 873 us: step_call(): pl.pallas_call(body, in_specs=[ANY] * 4, out_specs=[ANY] * 3 + [pl.BlockS...]
    ppermute x18 -> x0, starting transfers between devices: 295 us -> none  [the longest x9 211 us: tick(): bwd_next = lax.ppermute(bwd_out, 'stage', bwd_perm)]
    ppermute x18 -> x0, waiting for transfers between devices: 203 us -> none  [the longest x9 142 us: tick(): fwd_next = lax.ppermute(fwd_out, 'stage', fwd_perm)]
    another operation x20 -> x0, loops' own time: 153 us -> none  [the longest x9 105 us: tick(): acc_list, bwd_out = lax.switch(branch_idx, branch_list, acc_list)]
    broadcast_in_dim x8 -> x0, local copies, waits for them, and re-layouts: 73.6 us -> none  [the longest x2 33.5 us: device_fn(): zero_up = jnp.zeros(up_loc.shape[1:], jnp.float32)]
    select_n x13 -> x0, other arithmetic: 33.4 us -> none  [the longest x9 21.2 us: tick(): jnp.where(from_data, lax.dynamic_index_in_dim(tokens_loc, f_micro, 0, kee...]
  transfers between devices with their start and end apart: 22 -> 0, of which waited for: 17 -> 0; matrix products, arithmetic and copies ran while one was open for 11% -> 0% of each run, Pallas kernels for 0% -> 0%
where the time goes in v1:
time: 903 us; the launch traced here: 901 us
  Pallas kernels  892 us (99%)
    pallas_call x1, Pallas kernels, step_call(): pl.pallas_call(body, in_specs=[ANY] * 4, out_specs=[ANY] * 3 + [pl.BlockS...  873 us
    pallas_call x1, Pallas kernels, final_call(): pl.pallas_call(final_kernel, grid_spec=pltpu.PrefetchScalarGridSpec(num_s...  18.2 us

profile of v1, /device:TPU:0, one launch (start us, length us, event | category | flops | bytes accessed | tf_op | source)
XLA Modules:
  0.0 900.8 jit_solution(17719743784734613056)
XLA Ops:
  0.6 873.3 %step.1 = (bf16[4,16,3,256,896]{4,3,2,1,0:T(8,128)(2,1)}, f32[6,2,608,896]{3,2,1,0:T(8,128)}, f32[6,4,112,1280]{3,2,1,0:T(8,128)}, f32[8,128]{1,0:T(8,128)}, f32...) custom-call(bf16[4,256,896]{2,1,0:T(8,128)(2,1)} %bitcast.5, ...), custom_call_target="tpu_custom_call" | custom-call | tf_op jit(solution)/shard_map/step/pallas_call | solution.py:625
  874.0 1.2 slice.3
  875.8 0.7 dynamic-slice_bitcast_fusion.scal
  876.5 0.0 copy-start
  876.5 4.9 copy-done
  881.4 18.2 %final.1 = (f32[2,3,608,896]{3,2,1,0:T(8,128)}, f32[2,3,112,4864]{3,2,1,0:T(8,128)}) custom-call(s32[24]{0:T(128)S(1)} %dynamic-slice_bitcast_fusion.scal, f32[6,2,608,896]{3,2,1,0:T(8,128)} %get-tuple-element.9.dd, f32[6,4,112,1280]{3,2,1,0:T(8,128)S(1)} %copy-done), custom_call_target="tpu_custom_call" | custom-call | tf_op jit(solution)/shard_map/final/pallas_call | solution.py:661
Async XLA Ops:
  876.5 4.9 copy-start
